TPU v7x, 32 devices: a whole 2x2x4 slice. The times are simulated.
32 devices in a mesh: rows: 4 (over y, x), feat: 8 (over z, core).
Axes of the slice: x: 2, y: 2, z: 4, core: 2. Of those that a mesh axis runs over, the one named last changes fastest.
Arguments:
- bins: int32 [256, 32768], P(None, ('rows', 'feat')), may hold values from 0 to 255
- leaf: int32 [32768], P(('rows', 'feat')), may hold values from 0 to 1
- grad: bfloat16 [32, 32768], P(None, ('rows', 'feat')), may hold values from -15.55 to 15.55
- hess: bfloat16 [32, 32768], P(None, ('rows', 'feat')), may hold values from 0.049804688 to 1
Outputs:
- gains: float32 [256, 2, 256], P(('rows', 'feat'))
- best: float32 [2], replicated
All inputs are finite; a program needn't handle non-finite values.
Results may differ from a plain program's by a relative error of at most 0.0003.
Values may be sent and summed in bfloat16 or wider, within the bound.
A program may use at most 128 MiB of HBM per device.

v0:
```python
import math
import jax
import jax.numpy as jnp
from jax import lax
from jax.sharding import PartitionSpec as P

F = 256
B = 256
LEAVES = 2


def leaf_weighted(both, leaf_row, leaves):
    nodes = jnp.arange(leaves, dtype=jnp.float32)[:, None]
    hot = (leaf_row.astype(jnp.float32) == nodes).astype(jnp.bfloat16)
    return (hot[:, None, :] * both[None, :, :]).reshape(leaves * both.shape[0], both.shape[1])


def bin_counts(codes, weighted, bin_total):
    levels = jnp.arange(bin_total, dtype=jnp.int32)
    onehot = (codes[:, :, None] == levels).astype(jnp.bfloat16)
    return jnp.einsum("frb,cr->fbc", onehot, weighted, preferred_element_type=jnp.float32)


def split_gains(hist, totals, outputs):
    count = hist.shape[0]
    cum = jnp.cumsum(hist, axis=1).reshape(count, B, LEAVES, 2, outputs)
    tot = totals.reshape(LEAVES, 2, outputs)
    left_grad = cum[:, :, :, 0, :]
    left_hess = cum[:, :, :, 1, :]
    all_grad = tot[:, 0, :]
    all_hess = tot[:, 1, :]
    right_grad = all_grad - left_grad
    right_hess = all_hess - left_hess
    score = (
        left_grad * left_grad / (left_hess + 1.0)
        + right_grad * right_grad / (right_hess + 1.0)
        - all_grad * all_grad / (all_hess + 1.0)
    )
    gains = 0.5 / outputs * jnp.sum(score, axis=-1)
    return jnp.transpose(gains, (0, 2, 1))


def shards(bins, leaf, grad, hess):
    outputs = grad.shape[0]
    shard = bins.shape[1]
    devices = lax.axis_size("rows") * lax.axis_size("feat")
    owned = F // devices
    both = jnp.concatenate([grad, hess], axis=0)
    leaf_row = leaf[None, :]
    weighted = leaf_weighted(both, leaf_row, LEAVES)
    columns = weighted.shape[0]
    codes_mine = lax.all_to_all(bins, ("rows", "feat"), split_axis=0, concat_axis=1, tiled=True)
    initial = jnp.zeros((owned, B, columns), jnp.float32)
    both_piece = lax.all_gather(both, ("rows", "feat"), axis=1, tiled=True)
    leaf_piece = lax.all_gather(leaf_row.astype(jnp.bfloat16), ("rows", "feat"), axis=1, tiled=True)
    length = both_piece.shape[1]
    width = math.gcd(length, 8 * shard)

    def step(index, total):
        offset = index * width
        part_codes = lax.dynamic_slice_in_dim(codes_mine, offset, width, 1)
        part_both = lax.dynamic_slice_in_dim(both_piece, offset, width, 1)
        part_leaf = lax.dynamic_slice_in_dim(leaf_piece, offset, width, 1)
        return total + bin_counts(part_codes, leaf_weighted(part_both, part_leaf, LEAVES), B)

    hist = lax.fori_loop(0, length // width, step, initial)
    totals = lax.psum(jnp.sum(weighted, axis=1, dtype=jnp.float32), ("rows", "feat"))
    gains = split_gains(hist, totals, outputs)
    best = lax.pmax(jnp.max(gains, axis=(0, 2)), ("rows", "feat"))
    return (gains, best)


def solution(mesh):
    return jax.shard_map(
        shards,
        mesh=mesh,
        in_specs=(
            P(None, ("rows", "feat")),
            P(("rows", "feat")),
            P(None, ("rows", "feat")),
            P(None, ("rows", "feat")),
        ),
        out_specs=(P(("rows", "feat"), None, None), P()),
        check_vma=False,
    )
```

profile of v0, /device:TPU:0, one launch (start us, length us, event | category | flops | bytes accessed | tf_op | source)
XLA Modules:
  0.0 226.1 jit_solution(3870619815995787336)
XLA Ops:
  7.2 0.0 all-gather.3.cloned.1.call-start
  7.2 0.8 constant_dynamic-update-slice_fusion.1
  8.1 0.8 constant_dynamic-update-slice_fusion
  8.9 0.6 copy-done
  9.5 0.0 all-gather.3.cloned.1.call-update
  9.6 7.3 %all-to-all-start = ((s32[32,8,1024]{2,1,0:T(8,128)}), s32[32,8,1024]{2,1,0:T(8,128)S(1)}, u32[]{:S(2)}, u32[]{:S(2)}) async-start(s32[32,8,1024]{2,1,0:T(8,128)} %bitcast.44), calls=%async_computation | async-start | bytes 2097152 | tf_op jit(solution)/shard_map/all_to_all | solution.py:52
  17.0 0.1 convert_reduce_fusion
  17.1 0.1 reshape.98
  17.2 60.4 %all-gather = bf16[32768]{0:T(1024)(128)(2,1)S(1)} all-gather(bf16[1024]{0:T(1024)(128)(2,1)S(1)} %get-tuple-element.128), channel_id=2, replica_groups=mesh['rows'=4,'feat'=8] {'rows','feat'}, dimensions={0}, use_global_device_ids=true | all-gather | bytes 67584 | tf_op jit(solution)/shard_map/all_gather | solution.py:55
  77.6 0.1 reshape.101
  77.6 37.5 %psum.7 = f32[2,2,32]{2,1,0:T(2,128)S(1)} all-reduce(f32[2,2,32]{2,1,0:T(2,128)S(1)} %reshape.98), channel_id=1, replica_groups=mesh['rows'=4,'feat'=8] {'rows','feat'}, use_global_device_ids=true, to_apply=%region_5.6 | all-reduce | flops 128 | bytes 1024 | tf_op jit(solution)/shard_map/psum | solution.py:67
  115.2 0.0 all-gather.3.cloned.1.call-done
  115.2 58.8 %while.14 = (s32[]{:T(128)}, f32[8,256,128]{2,1,0:T(8,128)}, s32[8,32768]{1,0:T(8,128)S(1)}, bf16[1,32768]{1,0:T(2,128)(2,1)S(1)}, bf16[64,32768]{1,0:T(8,128)(2...) while((s32[]{:T(128)}, f32[8,256,128]{2,1,0:T(8,128)}, s32[8,32768]{1,0:T(8,128)S(1)}, ...), condition=%wide.region_1.0_spmd.clone, body=%wide.region_0.0_spmd.clone.sunk | while | flops 4313358336 | bytes 10371233 | solution.py:66
  115.2 1.3 constant_dynamic-slice_fusion.4
  116.6 0.2 broadcast_multiply_fusion.2
  116.8 12.3 %fusion.12 = f32[8,256,128]{2,1,0:T(8,128)} fusion(bf16[128,8192,1]{1,0,2:T(8,128)(2,1)S(1)} %bitcast.39, s32[8,8192]{1,0:T(8,128)S(1)} %constant_dynamic-slice_fusion.5, f32[8,256,128]{2,1,0:T(8,128)} %get-tuple-element.172, pred[]{:T(512)S(6)} %compare.3), kind=kOutput, calls=%fused_computation.3.clone.1 | convolution fusion | flops 4312268800 | bytes 4456449 | tf_op jit(solution)/shard_map/while/body/eval_jaxpr/frb,cr->fbc/dot_general | solution.py:21
  129.2 1.3 constant_dynamic-slice_fusion.4
  130.6 0.2 broadcast_multiply_fusion.2
  130.8 13.3 %fusion.12 = f32[8,256,128]{2,1,0:T(8,128)} fusion(bf16[128,8192,1]{1,0,2:T(8,128)(2,1)S(1)} %bitcast.39, s32[8,8192]{1,0:T(8,128)S(1)} %constant_dynamic-slice_fusion.5, f32[8,256,128]{2,1,0:T(8,128)} %get-tuple-element.172, pred[]{:T(512)S(6)} %compare.3), kind=kOutput, calls=%fused_computation.3.clone.1 | convolution fusion | flops 4312268800 | bytes 4456449 | tf_op jit(solution)/shard_map/while/body/eval_jaxpr/frb,cr->fbc/dot_general | solution.py:21
  144.1 1.3 constant_dynamic-slice_fusion.4
  145.5 0.2 broadcast_multiply_fusion.2
  145.7 13.4 %fusion.12 = f32[8,256,128]{2,1,0:T(8,128)} fusion(bf16[128,8192,1]{1,0,2:T(8,128)(2,1)S(1)} %bitcast.39, s32[8,8192]{1,0:T(8,128)S(1)} %constant_dynamic-slice_fusion.5, f32[8,256,128]{2,1,0:T(8,128)} %get-tuple-element.172, pred[]{:T(512)S(6)} %compare.3), kind=kOutput, calls=%fused_computation.3.clone.1 | convolution fusion | flops 4312268800 | bytes 4456449 | tf_op jit(solution)/shard_map/while/body/eval_jaxpr/frb,cr->fbc/dot_general | solution.py:21
  159.1 1.3 constant_dynamic-slice_fusion.4
  160.4 0.2 broadcast_multiply_fusion.2
  160.6 13.4 %fusion.12 = f32[8,256,128]{2,1,0:T(8,128)} fusion(bf16[128,8192,1]{1,0,2:T(8,128)(2,1)S(1)} %bitcast.39, s32[8,8192]{1,0:T(8,128)S(1)} %constant_dynamic-slice_fusion.5, f32[8,256,128]{2,1,0:T(8,128)} %get-tuple-element.172, pred[]{:T(512)S(6)} %compare.3), kind=kOutput, calls=%fused_computation.3.clone.1 | convolution fusion | flops 4312268800 | bytes 4456449 | tf_op jit(solution)/shard_map/while/body/eval_jaxpr/frb,cr->fbc/dot_general | solution.py:21
  174.0 1.8 fusion.3
  175.8 0.1 fusion.5
  175.9 0.1 broadcast_add_fusion
  176.0 0.4 copy.15
  176.4 0.4 subtract_reduce_fusion
  176.8 0.7 multiply_reduce_fusion
  177.5 41.8 %pmax.7 = f32[2]{0:T(128)} all-reduce(f32[2]{0:T(128)S(1)} %get-tuple-element.125), channel_id=1, replica_groups=mesh['rows'=4,'feat'=8] {'rows','feat'}, use_global_device_ids=true, to_apply=%region_8.9 | all-reduce | flops 2 | bytes 16 | tf_op jit(solution)/shard_map/pmax | solution.py:69
  (24 shorter events, 0.5 us)
Async XLA Ops:
  7.2 9.8 %copy-start.2 = (s32[1024]{0:T(1024)S(1)}, s32[1024]{0:T(1024)}, u32[]{:S(2)}) copy-start(s32[1024]{0:T(1024)} %param.7) | copy-start | bytes 12292
  7.2 108.0 %all-gather.3.cloned.1.call-start = ((), (), s32[]{:S(2)}) async-start(), calls=%async_computation.1 | async-start | bytes 4325376 | tf_op jit(solution)/shard_map/all_gather | solution.py:54
  8.9 0.6 copy-start
  9.6 7.4 %copy-start.1 = (bf16[64,1024]{1,0:T(8,128)(2,1)S(1)}, bf16[64,1024]{1,0:T(8,128)(2,1)}, u32[]{:S(2)}) copy-start(bf16[64,1024]{1,0:T(8,128)(2,1)} %copy-done) | copy-start | bytes 393220
  9.6 105.6 %all-to-all-start = ((s32[32,8,1024]{2,1,0:T(8,128)}), s32[32,8,1024]{2,1,0:T(8,128)S(1)}, u32[]{:S(2)}, u32[]{:S(2)}) async-start(s32[32,8,1024]{2,1,0:T(8,128)} %bitcast.44), calls=%async_computation | async-start | bytes 2097152 | tf_op jit(solution)/shard_map/all_to_all | solution.py:52
Sparse Core Ops, SparseCore 0:
  11.0 66.5 all-gather.2
where the time goes:
time: 227 us; the launch traced here: 226 us
  blocking collectives  140 us (62%)
  matrix products  52.4 us (23%)
  between operations  14.1 us (6%)
  local copies, waits for them, and re-layouts  8.17 us (4%)
  starting transfers between devices  7.37 us (3%)
  other arithmetic  4.15 us (2%)
    all_gather x1, blocking collectives, shards(): lax.all_gather(leaf_row.astype(jnp.bfloat16), ('rows', 'feat'), axis=1, t...  60.4 us
    dot_general x4, matrix products, bin_counts(): jnp.einsum('frb,cr->fbc', onehot, weighted, preferred_element_type=jnp.fl...  52.4 us
    pmax x1, blocking collectives, shards(): best = lax.pmax(jnp.max(gains, axis=(0, 2)), ('rows', 'feat'))  41.8 us
    psum x1, blocking collectives, shards(): lax.psum(jnp.sum(weighted, axis=1, dtype=jnp.float32), ('rows', 'feat'))  37.5 us
    all_to_all x1, starting transfers between devices, shards(): lax.all_to_all(bins, ('rows', 'feat'), split_axis=0, concat_axis=1, tiled...  7.33 us
    dynamic_slice x4, local copies, waits for them, and re-layouts, step(): part_both = lax.dynamic_slice_in_dim(both_piece, offset, width, 1)  5.17 us
  transfers between devices with their start and end apart: 2, of which 0 were waited for; matrix products, arithmetic and copies ran while one was open for 0% of the time, Pallas kernels for 0%

commit v1 on v0

--- a/solution.py
+++ b/solution.py
@@ -64,7 +64,8 @@
         return total + bin_counts(part_codes, leaf_weighted(part_both, part_leaf, LEAVES), B)
 
     hist = lax.fori_loop(0, length // width, step, initial)
-    totals = lax.psum(jnp.sum(weighted, axis=1, dtype=jnp.float32), ("rows", "feat"))
+    arr_in = jnp.sum(weighted, axis=1, dtype=jnp.float32)
+    totals = jnp.sum(lax.all_gather(arr_in, ("rows", "feat")), 0)
     gains = split_gains(hist, totals, outputs)
     best = lax.pmax(jnp.max(gains, axis=(0, 2)), ("rows", "feat"))
     return (gains, best)

time: 227 us -> 223 us (0.982)
  blocking collectives: 140 us -> 136 us
    all_gather x0 -> x1, blocking collectives: none -> 59.8 us  [shards(): totals = jnp.sum(lax.all_gather(arr_in, ('rows', 'feat')), 0)]
    psum x1 -> x0, blocking collectives: 37.5 us -> none  [shards(): lax.psum(jnp.sum(weighted, axis=1, dtype=jnp.float32), ('rows', 'feat'))]
    all_gather x1, blocking collectives: 60.4 us -> 36.9 us  [shards(): lax.all_gather(leaf_row.astype(jnp.bfloat16), ('rows', 'feat'), axis=1, t...]
    pmax x1, blocking collectives: 41.8 us -> 39.3 us  [shards(): best = lax.pmax(jnp.max(gains, axis=(0, 2)), ('rows', 'feat'))]
where the time goes in v1:
time: 223 us
  blocking collectives  136 us (61%)
  matrix products  52.4 us (23%)
  between operations  14.2 us (6%)
  local copies, waits for them, and re-layouts  8.26 us (4%)
  starting transfers between devices  7.37 us (3%)
  other arithmetic  4.2 us (2%)
    all_gather x1, blocking collectives, shards(): totals = jnp.sum(lax.all_gather(arr_in, ('rows', 'feat')), 0)  59.8 us
    dot_general x4, matrix products, bin_counts(): jnp.einsum('frb,cr->fbc', onehot, weighted, preferred_element_type=jnp.fl...  52.4 us
    pmax x1, blocking collectives, shards(): best = lax.pmax(jnp.max(gains, axis=(0, 2)), ('rows', 'feat'))  39.3 us
    all_gather x1, blocking collectives, shards(): lax.all_gather(leaf_row.astype(jnp.bfloat16), ('rows', 'feat'), axis=1, t...  36.9 us
    all_to_all x1, starting transfers between devices, shards(): lax.all_to_all(bins, ('rows', 'feat'), split_axis=0, concat_axis=1, tiled...  7.33 us
    dynamic_slice x4, local copies, waits for them, and re-layouts, step(): part_both = lax.dynamic_slice_in_dim(both_piece, offset, width, 1)  5.17 us
  transfers between devices with their start and end apart: 2, of which 0 were waited for; matrix products, arithmetic and copies ran while one was open for 0% of the time, Pallas kernels for 0%

profile of v1, /device:TPU:0, one launch (start us, length us, event | category | flops | bytes accessed | tf_op | source)
XLA Modules:
  0.0 222.6 jit_solution(5283076173714647127)
XLA Ops:
  7.2 0.0 all-gather.4.cloned.1.call-start
  7.2 0.8 constant_dynamic-update-slice_fusion.1
  8.1 0.8 constant_dynamic-update-slice_fusion
  8.9 0.6 copy-done
  9.6 7.3 %all-to-all-start = ((s32[32,8,1024]{2,1,0:T(8,128)}), s32[32,8,1024]{2,1,0:T(8,128)S(1)}, u32[]{:S(2)}, u32[]{:S(2)}) async-start(s32[32,8,1024]{2,1,0:T(8,128)} %bitcast.44), calls=%async_computation | async-start | bytes 2097152 | tf_op jit(solution)/shard_map/all_to_all | solution.py:52
  17.0 0.1 convert_reduce_fusion
  17.1 0.1 reshape.102
  17.2 59.8 %all-gather.1 = f32[32,1,128]{2,1,0:T(1,128)S(1)} all-gather(f32[1,1,128]{2,1,0:T(1,128)S(1)} %reshape.102), channel_id=1, replica_groups=mesh['rows'=4,'feat'=8] {'rows','feat'}, dimensions={0}, use_global_device_ids=true | all-gather | bytes 16896 | tf_op jit(solution)/shard_map/all_gather | solution.py:68
  77.0 0.1 reduce_sum.28
  77.1 0.1 reshape.99
  77.2 36.9 %all-gather = bf16[32768]{0:T(1024)(128)(2,1)S(1)} all-gather(bf16[1024]{0:T(1024)(128)(2,1)S(1)} %get-tuple-element.128), channel_id=2, replica_groups=mesh['rows'=4,'feat'=8] {'rows','feat'}, dimensions={0}, use_global_device_ids=true | all-gather | bytes 67584 | tf_op jit(solution)/shard_map/all_gather | solution.py:55
  114.1 0.1 reshape.101
  114.2 58.8 %while.14 = (s32[]{:T(128)}, f32[8,256,128]{2,1,0:T(8,128)}, s32[8,32768]{1,0:T(8,128)S(1)}, bf16[1,32768]{1,0:T(2,128)(2,1)S(1)}, bf16[64,32768]{1,0:T(8,128)(2...) while((s32[]{:T(128)}, f32[8,256,128]{2,1,0:T(8,128)}, s32[8,32768]{1,0:T(8,128)S(1)}, ...), condition=%wide.region_1.0_spmd.clone, body=%wide.region_0.0_spmd.clone.sunk | while | flops 4313358336 | bytes 10371233 | solution.py:66
  114.2 1.3 constant_dynamic-slice_fusion.4
  115.6 0.2 broadcast_multiply_fusion.2
  115.8 12.3 %fusion.12 = f32[8,256,128]{2,1,0:T(8,128)} fusion(bf16[128,8192,1]{1,0,2:T(8,128)(2,1)S(1)} %bitcast.39, s32[8,8192]{1,0:T(8,128)S(1)} %constant_dynamic-slice_fusion.5, f32[8,256,128]{2,1,0:T(8,128)} %get-tuple-element.172, pred[]{:T(512)S(6)} %compare.3), kind=kOutput, calls=%fused_computation.3.clone.1 | convolution fusion | flops 4312268800 | bytes 4456449 | tf_op jit(solution)/shard_map/while/body/eval_jaxpr/frb,cr->fbc/dot_general | solution.py:21
  128.1 1.3 constant_dynamic-slice_fusion.4
  129.5 0.2 broadcast_multiply_fusion.2
  129.7 13.4 %fusion.12 = f32[8,256,128]{2,1,0:T(8,128)} fusion(bf16[128,8192,1]{1,0,2:T(8,128)(2,1)S(1)} %bitcast.39, s32[8,8192]{1,0:T(8,128)S(1)} %constant_dynamic-slice_fusion.5, f32[8,256,128]{2,1,0:T(8,128)} %get-tuple-element.172, pred[]{:T(512)S(6)} %compare.3), kind=kOutput, calls=%fused_computation.3.clone.1 | convolution fusion | flops 4312268800 | bytes 4456449 | tf_op jit(solution)/shard_map/while/body/eval_jaxpr/frb,cr->fbc/dot_general | solution.py:21
  143.1 1.3 constant_dynamic-slice_fusion.4
  144.5 0.2 broadcast_multiply_fusion.2
  144.7 13.4 %fusion.12 = f32[8,256,128]{2,1,0:T(8,128)} fusion(bf16[128,8192,1]{1,0,2:T(8,128)(2,1)S(1)} %bitcast.39, s32[8,8192]{1,0:T(8,128)S(1)} %constant_dynamic-slice_fusion.5, f32[8,256,128]{2,1,0:T(8,128)} %get-tuple-element.172, pred[]{:T(512)S(6)} %compare.3), kind=kOutput, calls=%fused_computation.3.clone.1 | convolution fusion | flops 4312268800 | bytes 4456449 | tf_op jit(solution)/shard_map/while/body/eval_jaxpr/frb,cr->fbc/dot_general | solution.py:21
  158.0 1.3 constant_dynamic-slice_fusion.4
  159.4 0.2 broadcast_multiply_fusion.2
  159.6 13.3 %fusion.12 = f32[8,256,128]{2,1,0:T(8,128)} fusion(bf16[128,8192,1]{1,0,2:T(8,128)(2,1)S(1)} %bitcast.39, s32[8,8192]{1,0:T(8,128)S(1)} %constant_dynamic-slice_fusion.5, f32[8,256,128]{2,1,0:T(8,128)} %get-tuple-element.172, pred[]{:T(512)S(6)} %compare.3), kind=kOutput, calls=%fused_computation.3.clone.1 | convolution fusion | flops 4312268800 | bytes 4456449 | tf_op jit(solution)/shard_map/while/body/eval_jaxpr/frb,cr->fbc/dot_general | solution.py:21
  173.0 1.8 fusion.3
  174.8 0.1 fusion.5
  174.9 0.1 broadcast_add_fusion
  175.0 0.4 copy.15
  175.4 0.4 subtract_reduce_fusion
  175.7 0.7 multiply_reduce_fusion
  176.5 39.3 %pmax.7 = f32[2]{0:T(128)} all-reduce(f32[2]{0:T(128)S(1)} %get-tuple-element.125), channel_id=1, replica_groups=mesh['rows'=4,'feat'=8] {'rows','feat'}, use_global_device_ids=true, to_apply=%region_8.9 | all-reduce | flops 2 | bytes 16 | tf_op jit(solution)/shard_map/pmax | solution.py:70
  (26 shorter events, 0.5 us)
Async XLA Ops:
  7.2 9.8 %copy-start.2 = (s32[1024]{0:T(1024)S(1)}, s32[1024]{0:T(1024)}, u32[]{:S(2)}) copy-start(s32[1024]{0:T(1024)} %param.7) | copy-start | bytes 12292
  7.2 107.0 %all-gather.4.cloned.1.call-start = ((), (), s32[]{:S(2)}) async-start(), calls=%async_computation.1 | async-start | bytes 4325376 | tf_op jit(solution)/shard_map/all_gather | solution.py:54
  8.9 0.6 copy-start
  9.6 7.4 %copy-start.1 = (bf16[64,1024]{1,0:T(8,128)(2,1)S(1)}, bf16[64,1024]{1,0:T(8,128)(2,1)}, u32[]{:S(2)}) copy-start(bf16[64,1024]{1,0:T(8,128)(2,1)} %copy-done) | copy-start | bytes 393220
  9.6 104.6 %all-to-all-start = ((s32[32,8,1024]{2,1,0:T(8,128)}), s32[32,8,1024]{2,1,0:T(8,128)S(1)}, u32[]{:S(2)}, u32[]{:S(2)}) async-start(s32[32,8,1024]{2,1,0:T(8,128)} %bitcast.44), calls=%async_computation | async-start | bytes 2097152 | tf_op jit(solution)/shard_map/all_to_all | solution.py:52
Sparse Core Ops, SparseCore 0:
  11.0 66.4 all-gather.3
